TPU v7x, 256 devices: a 8x8x2 block of a 8x8x16 slice. The times are simulated.
256 devices in a mesh: groups: 2 (over z), seq: 64 (over x, y), mp: 2 (over core).
Axes of the slice: x: 8, y: 8, z: 2, core: 2. Of those that a mesh axis runs over, the one named last changes fastest.
The devices are a block of a 8x8x16 slice.
Arguments:
- latent_cache: bfloat16 [16384, 64, 512], P(('groups', 'seq')), parts along dimension 0, may hold values from -6 to 6
- rope_cache: bfloat16 [16384, 4096], P(('groups', 'seq')), parts along dimension 0, may hold values from -6 to 6
- q_nope: bfloat16 [16, 128, 128], P('groups', 'mp'), parts along dimension 0, may hold values from -12 to 12
- q_rope: bfloat16 [16, 128, 64], P('groups', 'mp'), parts along dimension 0, may hold values from -2000 to 2000
- w_uk: bfloat16 [128, 128, 512], P('mp', None, 'seq'), may hold values from -0.5 to 0.5
- value_up_weight: bfloat16 [128, 512, 128], P('mp', 'seq'), may hold values from -0.25 to 0.25
- w_out: bfloat16 [16384, 7168], P('mp', 'seq'), may hold values from -0.046875 to 0.046875
- page_table: int32 [16, 2048], P('groups'), parts along dimension 0, may hold values from 0 to 8191, as said below
- lengths: int32 [16], P('groups'), parts along dimension 0, may hold values from 16384 to 131072, as said below
Outputs:
- output: bfloat16 [16, 7168], P('groups', ('seq', 'mp')), parts along dimension 0
There are 2 independent parts, one for each index of `groups`. A program takes and returns all parts, laid end to end along the dimension named above; an argument that names none is the same for every part. Nothing has to cross between parts.
Inputs may be any that keep to these rules, and one draw needn't show every extreme that they name: `lengths`: every sequence has one eighth of 131072 tokens or more; the longest has exactly 131072. page_table[b,p] for p < ceil(lengths[b] / 64) is the global slot (shard index times 128 plus local slot) holding that page; these live entries are all distinct; the other entries are 0 and unused.
All inputs are finite; a program needn't handle non-finite values.
Results may differ from a plain program's by a relative error of at most 0.012.
Values may be sent and summed in bfloat16 or wider, within the bound.
A program may use at most 64 MiB of HBM per device.

v0:
```python
import jax
import jax.numpy as jnp
from jax import lax
from jax.sharding import Mesh
from jax.sharding import PartitionSpec as P

SEQ = ("seq_0", "seq_1")
GROUPS_SEQ = ("groups", "seq_0", "seq_1")
SEQ_MP = ("seq_0", "seq_1", "mp")
NEG = -1e30


def laid_out(tiles, dim):
    tiles = jnp.moveaxis(tiles, 0, dim)
    lengths = tiles.shape
    return tiles.reshape(*lengths[:dim], lengths[dim] * lengths[dim + 1], *lengths[dim + 2 :])


def from_everyone(x, axis):
    size = lax.axis_size(axis)
    return lax.all_to_all(jnp.broadcast_to(x[None], (size, *x.shape)), axis, 0, 0, tiled=True)


def collect(x, axis, dim):
    return laid_out(from_everyone(x, axis), dim)


def side_by_side(arrays, axis, split_dim, concat_dim, along):
    ends, at = ([], 0)
    for a in arrays[:-1]:
        at += a.shape[along]
        ends.append(at)
    both = jnp.concatenate(arrays, axis=along)
    return tuple(
        jnp.split(
            lax.all_to_all(both, axis, split_axis=split_dim, concat_axis=concat_dim, tiled=True),
            ends,
            axis=along,
        )
    )


def by_axis(x, axes):
    for axis in axes:
        x = lax.psum(x, axis)
    return x


def cut_along(x, dim, size):
    lengths = x.shape
    tiles = x.reshape(*lengths[:dim], size, lengths[dim] // size, *lengths[dim + 1 :])
    return jnp.moveaxis(tiles, dim, 0)


def sum_at_owner(x, axis, dim):
    size = lax.axis_size(axis)
    tiles = lax.all_to_all(cut_along(x, dim, size), axis, 0, 0, tiled=True)
    return jnp.sum(tiles, axis=0)


def local(
    latent_cache, rope_cache, q_nope, q_rope, w_uk, value_up_weight, w_out, page_table, lengths
):
    slots_dev, page_len, latent_width = latent_cache.shape
    rope_width = q_rope.shape[2]
    seq_count, heads = (q_nope.shape[0], q_nope.shape[1])
    score_scale = (q_nope.shape[2] + rope_width) ** (-0.5)
    q_part = jnp.einsum("bhn,hnk->bhk", q_nope, w_uk, preferred_element_type=jnp.float32).astype(
        jnp.bfloat16
    )
    q_latent = collect(q_part, SEQ, 2)
    first_slot = lax.axis_index(SEQ) * slots_dev
    page_count = (lengths + page_len - 1) // page_len
    logical = jnp.arange(page_table.shape[1], dtype=jnp.int32)
    live_page = logical[None, :] < page_count[:, None]
    tokens_in = jnp.clip(lengths[:, None] - page_len * logical[None, :], 0, page_len)
    local_ids = jnp.arange(slots_dev, dtype=jnp.int32)
    hits = ((page_table - first_slot)[:, :, None] == local_ids[None, None, :]) & live_page[
        :, :, None
    ]
    owner_mask = jnp.any(hits, axis=1)
    slot_fill = jnp.sum(jnp.where(hits, tokens_in[:, :, None], 0), axis=(0, 1))
    owner_half = owner_mask.astype(jnp.bfloat16)

    def update(run_state, index):
        run_max, run_sum, run_out = run_state
        start = index * 8
        latent_block = lax.dynamic_slice_in_dim(latent_cache, start, 8, 0)
        rope_block = lax.dynamic_slice_in_dim(rope_cache, start, 8, 0).reshape(
            8, page_len, rope_width
        )
        owner_block = lax.dynamic_slice_in_dim(owner_half, start, 8, 1)
        fill_block = lax.dynamic_slice_in_dim(slot_fill, start, 8, 0)
        pick_latent = jnp.einsum(
            "bs,bhk->shk", owner_block, q_latent, preferred_element_type=jnp.float32
        ).astype(jnp.bfloat16)
        pick_rope = jnp.einsum(
            "bs,bhr->shr", owner_block, q_rope, preferred_element_type=jnp.float32
        ).astype(jnp.bfloat16)
        scores = (
            jnp.einsum(
                "shk,stk->sht", pick_latent, latent_block, preferred_element_type=jnp.float32
            )
            + jnp.einsum("shr,str->sht", pick_rope, rope_block, preferred_element_type=jnp.float32)
        ) * score_scale
        live_token = (
            jnp.arange(page_len, dtype=jnp.int32)[None, None, :] < fill_block[:, None, None]
        )
        slot_max = jnp.max(jnp.where(live_token, scores, NEG), axis=2)
        exponent = jnp.where(live_token, jnp.exp(scores - slot_max[:, :, None]), 0.0)
        slot_sum = jnp.sum(exponent, axis=2)
        slot_out = jnp.einsum(
            "sht,stk->shk",
            exponent.astype(jnp.bfloat16),
            latent_block,
            preferred_element_type=jnp.float32,
        )
        owned = owner_block > 0
        candidate = jnp.where(owned[:, :, None], slot_max[None, :, :], NEG)
        new_max = jnp.maximum(run_max, jnp.max(candidate, axis=1))
        carry_scale = jnp.exp(run_max - new_max)
        factor = jnp.where(owned[:, :, None], jnp.exp(candidate - new_max[:, None, :]), 0.0)
        run_sum = run_sum * carry_scale + jnp.einsum("bsh,sh->bh", factor, slot_sum)
        run_out = run_out * carry_scale[:, :, None] + jnp.einsum("bsh,shk->bhk", factor, slot_out)
        return (new_max, run_sum, run_out)

    def visit(index, run_state):
        return update(run_state, index)

    initial = (
        jnp.full((seq_count, heads), NEG, jnp.float32),
        jnp.zeros((seq_count, heads), jnp.float32),
        jnp.zeros((seq_count, heads, latent_width), jnp.float32),
    )
    run_max, run_sum, run_out = lax.fori_loop(0, slots_dev // 8, visit, initial)
    share_width = value_up_weight.shape[1]
    shards = lax.axis_size(SEQ)
    spread_max = jnp.broadcast_to(run_max[:, :, None], (seq_count, heads, shards))
    spread_sum = jnp.broadcast_to(run_sum[:, :, None], (seq_count, heads, shards))
    peers_max, peers_sum, peers_out = (
        *side_by_side((spread_max, spread_sum), SEQ, 2, 2, 0),
        lax.all_to_all(run_out, SEQ, split_axis=2, concat_axis=2, tiled=True),
    )
    top = jnp.max(peers_max, axis=2)
    rescale = jnp.exp(peers_max - top[:, :, None])
    totals = jnp.sum(peers_sum * rescale, axis=2)
    grouped = peers_out.reshape(seq_count, heads, shards, share_width)
    shared_latent = jnp.sum(grouped * rescale[:, :, :, None], axis=2)
    local_portion = (shared_latent / totals[:, :, None]).astype(jnp.bfloat16)
    value_slice = jnp.einsum(
        "gre,req->grq", local_portion, value_up_weight, preferred_element_type=jnp.float32
    )
    value_rows = by_axis(value_slice, SEQ).astype(jnp.bfloat16)
    flat_values = value_rows.reshape(seq_count, heads * value_rows.shape[2])
    partial_out = jnp.dot(flat_values, w_out, preferred_element_type=jnp.float32)
    return sum_at_owner(partial_out, "mp", 1).astype(jnp.bfloat16)


def solution(mesh):
    finer = Mesh(
        mesh.devices.reshape(mesh.shape["groups"], 8, 8, mesh.shape["mp"]),
        ("groups", "seq_0", "seq_1", "mp"),
    )
    return jax.shard_map(
        local,
        mesh=finer,
        in_specs=(
            P(GROUPS_SEQ, None, None),
            P(GROUPS_SEQ, None),
            P("groups", "mp", None),
            P("groups", "mp", None),
            P("mp", None, SEQ),
            P("mp", SEQ, None),
            P("mp", SEQ),
            P("groups", None),
            P("groups"),
        ),
        out_specs=P("groups", SEQ_MP),
        check_vma=False,
    )
```

profile of v0, /device:TPU:513, one launch (start us, length us, event | category | flops | bytes accessed | tf_op | source)
XLA Modules:
  0.0 388.7 jit_solution(2890915873763073449)
XLA Ops:
  8.3 1.6 reshape.114
  9.8 21.8 %all-to-all-start = ((bf16[64,2,2048]{2,1,0:T(2,128)(2,1)}), bf16[64,2,2048]{2,1,0:T(2,128)(2,1)}, u32[]{:S(2)}, u32[]{:S(2)}) async-start(bf16[64,2,2048]{2,1,0:T(2,128)(2,1)} %reshape.114), calls=%async_computation | async-start | bytes 1048576 | tf_op jit(solution)/shard_map/all_to_all | solution.py:21
  31.9 5.7 %fusion.41 = pred[8,128]{1,0:T(8,128)(4,1)S(1)} fusion(s32[8,2048]{1,0:T(8,128)S(1)} %get-tuple-element.269, pred[8,2048]{1,0:T(8,128)(4,1)S(1)} %iota_compare_fusion.2), kind=kLoop, calls=%fused_computation.56 | loop fusion | flops 6290432 | bytes 82944 | tf_op jit(solution)/shard_map/reduce_or | solution.py:81
  37.7 7.8 %select_reduce_fusion.2 = s32[128]{0:T(128)S(1)} fusion(s32[8,2048]{1,0:T(8,128)S(1)} %get-tuple-element.268, s32[8,2048]{1,0:T(8,128)S(1)} %get-tuple-element.269, pred[8,2048]{1,0:T(8,128)(4,1)S(1)} %iota_compare_fusion.2), kind=kLoop, calls=%fused_computation.53 | loop fusion | flops 8388480 | bytes 147968 | tf_op jit(solution)/shard_map/reduce_sum | solution.py:82
  45.5 2.3 reshape.115
  49.1 1.9 copy.48
  51.0 138.7 %while.18 = (s32[]{:T(128)}, f32[8,64]{0,1:T(8,128)S(1)}, f32[8,64]{0,1:T(8,128)S(1)}, f32[8,64,512]{2,0,1:T(8,128)}, bf16[8,128]{1,0:T(8,128)(2,1)S(1)}, /*inde...) while((s32[]{:T(128)}, f32[8,64]{0,1:T(8,128)S(1)}, ...), condition=%wide.region_6.7_spmd.clone, body=%wide.region_2.6_spmd.clone.sunk | while | flops 81668672 | bytes 7003699 | solution.py:135
  51.4 1.4 fusion.89
  54.5 1.5 fusion.93
  57.0 1.5 fusion.94
  62.0 1.5 fusion.93
  64.5 2.7 fusion.94
  67.7 1.4 fusion.89
  70.7 1.5 fusion.93
  73.3 2.7 fusion.94
  76.4 1.4 fusion.89
  79.5 1.5 fusion.93
  82.0 2.7 fusion.94
  85.2 1.4 fusion.89
  88.2 1.5 fusion.93
  90.8 2.7 fusion.94
  93.9 1.4 fusion.89
  97.0 1.5 fusion.93
  99.5 2.7 fusion.94
  102.7 1.4 fusion.89
  105.7 1.5 fusion.93
  108.2 2.7 fusion.94
  111.4 1.4 fusion.89
  114.4 1.5 fusion.93
  117.0 2.7 fusion.94
  120.1 1.4 fusion.89
  123.2 1.5 fusion.93
  125.7 2.7 fusion.94
  128.9 1.4 fusion.89
  131.9 1.5 fusion.93
  134.5 2.7 fusion.94
  137.6 1.4 fusion.89
  140.7 1.5 fusion.93
  143.2 2.7 fusion.94
  146.4 1.4 fusion.89
  149.4 1.5 fusion.93
  151.9 2.7 fusion.94
  158.1 1.5 fusion.93
  160.7 2.7 fusion.94
  163.9 1.4 fusion.89
  166.9 1.5 fusion.93
  169.4 2.7 fusion.94
  175.6 1.5 fusion.93
  178.2 2.7 fusion.94
  181.3 1.4 fusion.89
  184.4 1.5 fusion.93
  186.9 2.7 fusion.94
  190.9 13.3 %all-to-all-start.2 = ((f32[64,1,1024]{2,1,0:T(1,128)}), f32[64,1,1024]{2,1,0:T(1,128)S(1)}, u32[]{:S(2)}, u32[]{:S(2)}) async-start(f32[64,1,1024]{2,1,0:T(1,128)} %reshape.118), calls=%async_computation.2 | async-start | bytes 524288 | tf_op jit(solution)/shard_map/all_to_all | solution.py:36
  204.3 2.3 copy.50
  206.6 3.4 reshape.116
  210.0 5.1 %all-to-all-done.2 = f32[64,1,1024]{2,1,0:T(1,128)S(1)} async-done(((f32[64,1,1024]{2,1,0:T(1,128)}), f32[64,1,1024]{2,1,0:T(1,128)S(1)}, u32[]{:S(2)}, u32[]{:S(2)}) %all-to-all-start.2) | async-done | bytes 262176 | tf_op jit(solution)/shard_map/all_to_all | solution.py:36
  215.2 7.9 %all-to-all-start.1 = ((f32[64,1,4096]{2,1,0:T(1,128)}), f32[64,1,4096]{2,1,0:T(1,128)}, u32[]{:S(2)}, u32[]{:S(2)}) async-start(f32[64,1,4096]{2,1,0:T(1,128)} %reshape.116), calls=%async_computation.1 | async-start | bytes 2097152 | tf_op jit(solution)/shard_map/all_to_all | solution.py:142
  225.3 18.9 %all-to-all-done.1 = f32[64,1,4096]{2,1,0:T(1,128)} async-done(((f32[64,1,4096]{2,1,0:T(1,128)}), f32[64,1,4096]{2,1,0:T(1,128)}, u32[]{:S(2)}, u32[]{:S(2)}) %all-to-all-start.1) | async-done | bytes 1048608 | tf_op jit(solution)/shard_map/all_to_all | solution.py:142
  244.2 4.4 %reduce = f32[64,4096]{1,0:T(8,128)S(1)} reduce(f32[64,1,4096]{2,1,0:T(1,128)} %all-to-all-done.1, f32[]{:T(128)} %broadcast.134), dimensions={1}, to_apply=%all_to_all.13.reduce_sub_computation | reduce | bytes 2097156 | tf_op jit(solution)/shard_map/all_to_all | solution.py:142
  248.6 2.2 reshape.117
  250.7 2.2 fusion.42
  254.1 82.6 %all-reduce.3.cloned.1.call-done = f32[8,64,128]{2,0,1:T(8,128)} async-done(((f32[8,64,128]{2,0,1:T(8,128)}), f32[8,64,128]{2,0,1:T(8,128)}) %all-reduce.3.cloned.1.call-update) | async-done | bytes 262160 | tf_op jit(solution)/shard_map/psum | solution.py:45
  336.7 26.8 %all-reduce.4 = bf16[8,64,128]{2,0,1:T(8,128)(2,1)S(1)} all-reduce(f32[8,64,128]{2,0,1:T(8,128)} %all-reduce.3.cloned.1.call-done), channel_id=1, replica_groups=mesh['groups'=2,'seq_0'=8,'seq_1'=8,'mp'=2] {'seq_1'}, use_global_device_ids=true, to_apply=%region_11.12 | all-reduce | flops 65536 | bytes 393216 | tf_op jit(solution)/shard_map/psum | solution.py:45
  364.5 16.0 %all_to_all.20 = f32[2,1,448]{2,1,0:T(1,128)S(1)} all-to-all(f32[2,1,448]{2,1,0:T(1,128)S(1)} %reshape.120), channel_id=1, replica_groups=mesh['groups'=2,'seq_0'=8,'seq_1'=8,'mp'=2] {'mp'}, dimensions={0} | all-to-all | bytes 7168 | tf_op jit(solution)/shard_map/all_to_all | solution.py:57
  (355 shorter events, 63.0 us)
Async XLA Ops:
  6.5 356.9 %copy-start = (bf16[8192,112]{0,1:T(8,128)(2,1)S(1)}, bf16[8192,112]{0,1:T(8,128)(2,1)}, u32[]{:S(2)}) copy-start(bf16[8192,112]{0,1:T(8,128)(2,1)} %param.17) | copy-start | bytes 5505028
  6.6 25.2 %copy-start.5 = (s32[8]{0:T(128)S(1)}, s32[8]{0:T(128)}, u32[]{:S(2)}) copy-start(s32[8]{0:T(128)} %param.19) | copy-start | bytes 100
  6.6 25.2 %copy-start.4 = (s32[8,2048]{1,0:T(8,128)S(1)}, s32[8,2048]{1,0:T(8,128)}, u32[]{:S(2)}) copy-start(s32[8,2048]{1,0:T(8,128)} %param.18) | copy-start | bytes 196612
  7.9 29.8 %copy-start.2 = (bf16[8,64,64]{2,1,0:T(8,128)(2,1)S(1)}, bf16[8,64,64]{2,1,0:T(8,128)(2,1)}, u32[]{:S(2)}) copy-start(bf16[8,64,64]{2,1,0:T(8,128)(2,1)} %param.14) | copy-start | bytes 196612
  9.8 35.7 %all-to-all-start = ((bf16[64,2,2048]{2,1,0:T(2,128)(2,1)}), bf16[64,2,2048]{2,1,0:T(2,128)(2,1)}, u32[]{:S(2)}, u32[]{:S(2)}) async-start(bf16[64,2,2048]{2,1,0:T(2,128)(2,1)} %reshape.114), calls=%async_computation | async-start | bytes 1048576 | tf_op jit(solution)/shard_map/all_to_all | solution.py:21
  189.6 14.6 %copy-start.1 = (f32[8,64,512]{2,0,1:T(8,128)S(1)}, f32[8,64,512]{2,0,1:T(8,128)}, u32[]{:S(2)}) copy-start(f32[8,64,512]{2,0,1:T(8,128)} %get-tuple-element.176) | copy-start | bytes 3145732
  190.9 24.2 %all-to-all-start.2 = ((f32[64,1,1024]{2,1,0:T(1,128)}), f32[64,1,1024]{2,1,0:T(1,128)S(1)}, u32[]{:S(2)}, u32[]{:S(2)}) async-start(f32[64,1,1024]{2,1,0:T(1,128)} %reshape.118), calls=%async_computation.2 | async-start | bytes 524288 | tf_op jit(solution)/shard_map/all_to_all | solution.py:36
  215.2 29.0 %all-to-all-start.1 = ((f32[64,1,4096]{2,1,0:T(1,128)}), f32[64,1,4096]{2,1,0:T(1,128)}, u32[]{:S(2)}, u32[]{:S(2)}) async-start(f32[64,1,4096]{2,1,0:T(1,128)} %reshape.116), calls=%async_computation.1 | async-start | bytes 2097152 | tf_op jit(solution)/shard_map/all_to_all | solution.py:142
  223.1 113.6 %all-reduce.3.cloned.1.call-start = ((), (), s32[]{:S(2)}) async-start(), calls=%async_computation.4 | async-start | bytes 524288 | tf_op jit(solution)/shard_map/psum | solution.py:45
  248.5 4.5 %copy-start.3 = (bf16[64,8,128]{2,1,0:T(8,128)(2,1)S(1)}, bf16[64,8,128]{2,1,0:T(8,128)(2,1)}, u32[]{:S(2)}) copy-start(bf16[64,8,128]{2,1,0:T(8,128)(2,1)} %param.16) | copy-start | bytes 393220
Sparse Core Ops, SparseCore 0:
  254.2 82.4 all-reduce.2
where the time goes:
time: 392 us; the launch traced here: 389 us
  matrix products  110 us (28%)
  waiting for transfers between devices  107 us (27%)
  starting transfers between devices  43.1 us (11%)
  blocking collectives  42.8 us (11%)
  local copies, waits for them, and re-layouts  42.3 us (11%)
  other arithmetic  29.5 us (8%)
  between operations  13.7 us (3%)
    psum x1, waiting for transfers between devices, by_axis(): x = lax.psum(x, axis)  82.6 us
    dot_general x16, matrix products, update(): jnp.einsum('bsh,shk->bhk', factor, slot_out)  42.6 us
    psum x1, blocking collectives, by_axis(): x = lax.psum(x, axis)  26.8 us
    dot_general x16, matrix products, update(): jnp.einsum('sht,stk->shk', exponent.astype(jnp.bfloat16), latent_block, p...  24.3 us
    dot_general x16, matrix products, update(): jnp.einsum('shk,stk->sht', pick_latent, latent_block, preferred_element_t...  22 us
    all_to_all x1, starting transfers between devices, from_everyone(): lax.all_to_all(jnp.broadcast_to(x[None], (size, *x.shape)), axis, 0, 0, t...  21.8 us
    all_to_all x1, waiting for transfers between devices, local(): lax.all_to_all(run_out, SEQ, split_axis=2, concat_axis=2, tiled=True)  18.9 us
    all_to_all x1, blocking collectives, sum_at_owner(): tiles = lax.all_to_all(cut_along(x, dim, size), axis, 0, 0, tiled=True)  16 us
  transfers between devices with their start and end apart: 4, of which 3 were waited for; matrix products, arithmetic and copies ran while one was open for 6% of the time, Pallas kernels for 0%

commit v1 on v0

--- a/solution.py
+++ b/solution.py
@@ -3,6 +3,7 @@
 from jax import lax
 from jax.sharding import Mesh
 from jax.sharding import PartitionSpec as P
+from jax.lax import all_gather
 
 SEQ = ("seq_0", "seq_1")
 GROUPS_SEQ = ("groups", "seq_0", "seq_1")
@@ -42,7 +43,7 @@
 
 def by_axis(x, axes):
     for axis in axes:
-        x = lax.psum(x, axis)
+        x = jnp.sum(all_gather(x, axis), axis=0)
     return x
 
 

time: 392 us -> 378 us (0.964)
  blocking collectives: 42.8 us -> 8.23 us
  waiting for transfers between devices: 107 us -> 123 us
    all_gather x0 -> x2, waiting for transfers between devices: none -> 98.4 us  [by_axis(): x = jnp.sum(all_gather(x, axis), axis=0)]
    psum x1 -> x0, waiting for transfers between devices: 82.6 us -> none  [by_axis(): x = lax.psum(x, axis)]
    psum x1 -> x0, blocking collectives: 26.8 us -> none  [by_axis(): x = lax.psum(x, axis)]
    all_to_all x1, blocking collectives: 16 us -> 8.23 us  [sum_at_owner(): tiles = lax.all_to_all(cut_along(x, dim, size), axis, 0, 0, tiled=True)]
  transfers between devices with their start and end apart: 4 -> 5, of which waited for: 3 -> 4; matrix products, arithmetic and copies ran while one was open for 6% -> 6% of each run, Pallas kernels for 0% -> 0%
where the time goes in v1:
time: 378 us; the launch traced here: 374 us
  waiting for transfers between devices  123 us (33%)
  matrix products  110 us (29%)
  starting transfers between devices  43.2 us (11%)
  local copies, waits for them, and re-layouts  43.1 us (11%)
  other arithmetic  33.1 us (9%)
  between operations  13.7 us (4%)
  blocking collectives  8.23 us (2%)
    all_gather x2, waiting for transfers between devices, by_axis(): x = jnp.sum(all_gather(x, axis), axis=0)  98.4 us
    dot_general x16, matrix products, update(): jnp.einsum('bsh,shk->bhk', factor, slot_out)  42.6 us
    dot_general x16, matrix products, update(): jnp.einsum('sht,stk->shk', exponent.astype(jnp.bfloat16), latent_block, p...  24.3 us
    dot_general x16, matrix products, update(): jnp.einsum('shk,stk->sht', pick_latent, latent_block, preferred_element_t...  22 us
    all_to_all x1, starting transfers between devices, from_everyone(): lax.all_to_all(jnp.broadcast_to(x[None], (size, *x.shape)), axis, 0, 0, t...  21.8 us
    all_to_all x1, waiting for transfers between devices, local(): lax.all_to_all(run_out, SEQ, split_axis=2, concat_axis=2, tiled=True)  18.9 us
    dynamic_slice x16, local copies, waits for them, and re-layouts, update(): lax.dynamic_slice_in_dim(rope_cache, start, 8, 0)  13.5 us
    all_to_all x1, starting transfers between devices, side_by_side(): lax.all_to_all(both, axis, split_axis=split_dim, concat_axis=concat_dim,...  13.3 us
  transfers between devices with their start and end apart: 5, of which 4 were waited for; matrix products, arithmetic and copies ran while one was open for 6% of the time, Pallas kernels for 0%

profile of v1, /device:TPU:513, one launch (start us, length us, event | category | flops | bytes accessed | tf_op | source)
XLA Modules:
  0.0 374.5 jit_solution(5219496305210417585)
XLA Ops:
  8.3 1.6 reshape.122
  9.8 21.8 %all-to-all-start = ((bf16[64,2,2048]{2,1,0:T(2,128)(2,1)}), bf16[64,2,2048]{2,1,0:T(2,128)(2,1)}, u32[]{:S(2)}, u32[]{:S(2)}) async-start(bf16[64,2,2048]{2,1,0:T(2,128)(2,1)} %reshape.122), calls=%async_computation | async-start | bytes 1048576 | tf_op jit(solution)/shard_map/all_to_all | solution.py:22
  31.9 5.7 %fusion.41 = pred[8,128]{1,0:T(8,128)(4,1)S(1)} fusion(s32[8,2048]{1,0:T(8,128)S(1)} %get-tuple-element.279, pred[8,2048]{1,0:T(8,128)(4,1)S(1)} %iota_compare_fusion.2), kind=kLoop, calls=%fused_computation.56 | loop fusion | flops 6290432 | bytes 82944 | tf_op jit(solution)/shard_map/reduce_or | solution.py:82
  37.7 7.8 %select_reduce_fusion.2 = s32[128]{0:T(128)S(1)} fusion(s32[8,2048]{1,0:T(8,128)S(1)} %get-tuple-element.278, s32[8,2048]{1,0:T(8,128)S(1)} %get-tuple-element.279, pred[8,2048]{1,0:T(8,128)(4,1)S(1)} %iota_compare_fusion.2), kind=kLoop, calls=%fused_computation.53 | loop fusion | flops 8388480 | bytes 147968 | tf_op jit(solution)/shard_map/reduce_sum | solution.py:83
  45.5 2.3 reshape.123
  49.1 1.9 copy.68
  51.0 138.7 %while.18 = (s32[]{:T(128)}, f32[8,64]{0,1:T(8,128)S(1)}, f32[8,64]{0,1:T(8,128)S(1)}, f32[8,64,512]{2,0,1:T(8,128)}, bf16[8,128]{1,0:T(8,128)(2,1)S(1)}, /*inde...) while((s32[]{:T(128)}, f32[8,64]{0,1:T(8,128)S(1)}, ...), condition=%wide.region_6.7_spmd.clone, body=%wide.region_2.6_spmd.clone.sunk | while | flops 81668672 | bytes 7003699 | solution.py:136
  51.4 1.4 fusion.88
  54.5 1.5 fusion.92
  57.0 1.5 fusion.93
  62.0 1.5 fusion.92
  64.5 2.7 fusion.93
  67.7 1.4 fusion.88
  70.7 1.5 fusion.92
  73.3 2.7 fusion.93
  76.4 1.4 fusion.88
  79.5 1.5 fusion.92
  82.0 2.7 fusion.93
  88.2 1.5 fusion.92
  90.8 2.7 fusion.93
  93.9 1.4 fusion.88
  97.0 1.5 fusion.92
  99.5 2.7 fusion.93
  105.7 1.5 fusion.92
  108.2 2.7 fusion.93
  111.4 1.4 fusion.88
  114.4 1.5 fusion.92
  117.0 2.7 fusion.93
  120.1 1.4 fusion.88
  123.2 1.5 fusion.92
  125.7 2.7 fusion.93
  128.9 1.4 fusion.88
  131.9 1.5 fusion.92
  134.5 2.7 fusion.93
  137.6 1.4 fusion.88
  140.7 1.5 fusion.92
  143.2 2.7 fusion.93
  146.4 1.4 fusion.88
  149.4 1.5 fusion.92
  151.9 2.7 fusion.93
  158.1 1.5 fusion.92
  160.7 2.7 fusion.93
  163.9 1.4 fusion.88
  166.9 1.5 fusion.92
  169.4 2.7 fusion.93
  175.6 1.5 fusion.92
  178.2 2.7 fusion.93
  181.3 1.4 fusion.88
  184.4 1.5 fusion.92
  186.9 2.7 fusion.93
  190.9 13.3 %all-to-all-start.2 = ((f32[64,1,1024]{2,1,0:T(1,128)}), f32[64,1,1024]{2,1,0:T(1,128)S(1)}, u32[]{:S(2)}, u32[]{:S(2)}) async-start(f32[64,1,1024]{2,1,0:T(1,128)} %reshape.126), calls=%async_computation.2 | async-start | bytes 524288 | tf_op jit(solution)/shard_map/all_to_all | solution.py:37
  204.3 2.3 copy.70
  206.6 3.4 reshape.124
  210.0 5.1 %all-to-all-done.2 = f32[64,1,1024]{2,1,0:T(1,128)S(1)} async-done(((f32[64,1,1024]{2,1,0:T(1,128)}), f32[64,1,1024]{2,1,0:T(1,128)S(1)}, u32[]{:S(2)}, u32[]{:S(2)}) %all-to-all-start.2) | async-done | bytes 262176 | tf_op jit(solution)/shard_map/all_to_all | solution.py:37
  215.2 7.9 %all-to-all-start.1 = ((f32[64,1,4096]{2,1,0:T(1,128)}), f32[64,1,4096]{2,1,0:T(1,128)}, u32[]{:S(2)}, u32[]{:S(2)}) async-start(f32[64,1,4096]{2,1,0:T(1,128)} %reshape.124), calls=%async_computation.1 | async-start | bytes 2097152 | tf_op jit(solution)/shard_map/all_to_all | solution.py:143
  225.3 18.9 %all-to-all-done.1 = f32[64,1,4096]{2,1,0:T(1,128)} async-done(((f32[64,1,4096]{2,1,0:T(1,128)}), f32[64,1,4096]{2,1,0:T(1,128)}, u32[]{:S(2)}, u32[]{:S(2)}) %all-to-all-start.1) | async-done | bytes 1048608 | tf_op jit(solution)/shard_map/all_to_all | solution.py:143
  244.2 4.4 %reduce = f32[64,4096]{1,0:T(8,128)S(1)} reduce(f32[64,1,4096]{2,1,0:T(1,128)} %all-to-all-done.1, f32[]{:T(128)} %broadcast.134), dimensions={1}, to_apply=%all_to_all.13.reduce_sub_computation | reduce | bytes 2097156 | tf_op jit(solution)/shard_map/all_to_all | solution.py:143
  248.6 2.2 reshape.125
  250.7 2.2 fusion.42
  254.2 56.2 %all-gather.5.cloned.1.call-done = f32[64,64,128]{2,0,1:T(8,128)} async-done(((f32[8,64,128]{2,0,1:T(8,128)}), f32[64,64,128]{2,0,1:T(8,128)}) %all-gather.5.cloned.1.call-update) | async-done | bytes 2097168 | tf_op jit(solution)/shard_map/all_gather | solution.py:46
  310.4 1.8 bitcast_reduce_fusion
  313.1 42.2 %all-gather.7.cloned.1.call-done = f32[64,64,128]{2,1,0:T(8,128)} async-done(((f32[8,64,128]{2,1,0:T(8,128)}), f32[64,64,128]{2,1,0:T(8,128)}) %all-gather.7.cloned.1.call-update) | async-done | bytes 2097168 | tf_op jit(solution)/shard_map/all_gather | solution.py:46
  355.2 1.8 reduce_sum.71
  358.1 8.2 %all_to_all.20 = f32[2,1,448]{2,1,0:T(1,128)S(1)} all-to-all(f32[2,1,448]{2,1,0:T(1,128)S(1)} %reshape.128), channel_id=1, replica_groups=mesh['groups'=2,'seq_0'=8,'seq_1'=8,'mp'=2] {'mp'}, dimensions={0} | all-to-all | bytes 7168 | tf_op jit(solution)/shard_map/all_to_all | solution.py:58
  (361 shorter events, 66.7 us)
Async XLA Ops:
  6.5 350.5 %copy-start = (bf16[8192,112]{0,1:T(8,128)(2,1)S(1)}, bf16[8192,112]{0,1:T(8,128)(2,1)}, u32[]{:S(2)}) copy-start(bf16[8192,112]{0,1:T(8,128)(2,1)} %param.17) | copy-start | bytes 5505028
  6.6 25.2 %copy-start.5 = (s32[8]{0:T(128)S(1)}, s32[8]{0:T(128)}, u32[]{:S(2)}) copy-start(s32[8]{0:T(128)} %param.19) | copy-start | bytes 100
  6.6 25.2 %copy-start.4 = (s32[8,2048]{1,0:T(8,128)S(1)}, s32[8,2048]{1,0:T(8,128)}, u32[]{:S(2)}) copy-start(s32[8,2048]{1,0:T(8,128)} %param.18) | copy-start | bytes 196612
  7.9 29.8 %copy-start.2 = (bf16[8,64,64]{2,1,0:T(8,128)(2,1)S(1)}, bf16[8,64,64]{2,1,0:T(8,128)(2,1)}, u32[]{:S(2)}) copy-start(bf16[8,64,64]{2,1,0:T(8,128)(2,1)} %param.14) | copy-start | bytes 196612
  9.8 35.7 %all-to-all-start = ((bf16[64,2,2048]{2,1,0:T(2,128)(2,1)}), bf16[64,2,2048]{2,1,0:T(2,128)(2,1)}, u32[]{:S(2)}, u32[]{:S(2)}) async-start(bf16[64,2,2048]{2,1,0:T(2,128)(2,1)} %reshape.122), calls=%async_computation | async-start | bytes 1048576 | tf_op jit(solution)/shard_map/all_to_all | solution.py:22
  189.6 14.6 %copy-start.1 = (f32[8,64,512]{2,0,1:T(8,128)S(1)}, f32[8,64,512]{2,0,1:T(8,128)}, u32[]{:S(2)}) copy-start(f32[8,64,512]{2,0,1:T(8,128)} %get-tuple-element.176) | copy-start | bytes 3145732
  190.9 24.2 %all-to-all-start.2 = ((f32[64,1,1024]{2,1,0:T(1,128)}), f32[64,1,1024]{2,1,0:T(1,128)S(1)}, u32[]{:S(2)}, u32[]{:S(2)}) async-start(f32[64,1,1024]{2,1,0:T(1,128)} %reshape.126), calls=%async_computation.2 | async-start | bytes 524288 | tf_op jit(solution)/shard_map/all_to_all | solution.py:37
  215.2 29.0 %all-to-all-start.1 = ((f32[64,1,4096]{2,1,0:T(1,128)}), f32[64,1,4096]{2,1,0:T(1,128)}, u32[]{:S(2)}, u32[]{:S(2)}) async-start(f32[64,1,4096]{2,1,0:T(1,128)} %reshape.124), calls=%async_computation.1 | async-start | bytes 2097152 | tf_op jit(solution)/shard_map/all_to_all | solution.py:143
  223.1 87.3 %all-gather.5.cloned.1.call-start = ((), (), s32[]{:S(2)}) async-start(), calls=%async_computation.4 | async-start | bytes 2359296 | tf_op jit(solution)/shard_map/all_gather | solution.py:46
  248.5 4.5 %copy-start.3 = (bf16[64,8,128]{2,1,0:T(8,128)(2,1)S(1)}, bf16[64,8,128]{2,1,0:T(8,128)(2,1)}, u32[]{:S(2)}) copy-start(bf16[64,8,128]{2,1,0:T(8,128)(2,1)} %param.16) | copy-start | bytes 393220
  254.1 101.1 %all-gather.7.cloned.1.call-start = ((), (), s32[]{:S(2)}) async-start(), calls=%async_computation.5 | async-start | bytes 2359296 | tf_op jit(solution)/shard_map/all_gather | solution.py:46
Sparse Core Ops, SparseCore 0:
  254.2 56.1 all-gather.4
  313.2 41.9 all-gather.6
